TPU v7x, 256 devices: a whole 4x4x8 slice. The times are simulated.
256 devices in a mesh: gx: 8 (over z), gy: 32 (over y, x, core).
Axes of the slice: x: 4, y: 4, z: 8, core: 2. Of those that a mesh axis runs over, the one named last changes fastest.
Arguments:
- substrates: float32 [8, 512, 512, 128], P(None, 'gx', 'gy'), may hold values from 0 to 2
- uptake: float32 [512, 512, 128], P('gx', 'gy'), may hold values from 0.5 to 2
- diffusion: float32 [8], replicated, may hold values from 0.1 to 0.15
- decay_rate: float32 [8], replicated, may hold values from 0.01 to 0.1
Outputs:
- advanced: float32 [8, 512, 512, 128], P(None, 'gx', 'gy')
All inputs are finite; a program needn't handle non-finite values.
Results may differ from a plain program's by a relative error of at most 0.00002.
Values sent between devices are 32-bit elements; how exact they have to be, the bound alone decides.
A program may use at most 128 MiB of HBM per device.

v0:
```python
import jax
import jax.numpy as jnp
from jax import lax
from jax.sharding import PartitionSpec as P

SUBSTEPS = 4


def extended(x, sides, width):
    edges = {}
    for axis, dim in sides:
        size, length = (lax.axis_size(axis), x.shape[dim])
        up = [(i, (i + 1) % size) for i in range(size)]
        last = lax.slice_in_dim(x, length - width, length, axis=dim)
        first = lax.slice_in_dim(x, 0, width, axis=dim)
        edges[dim] = (
            lax.ppermute(last, axis, up),
            lax.ppermute(first, axis, [(b, a) for a, b in up]),
        )
    done = []
    for _, dim in sides:
        low, high = edges[dim]
        around = [(width, width) if d in done else (0, 0) for d in range(x.ndim)]
        x = jnp.concatenate([jnp.pad(low, around), x, jnp.pad(high, around)], axis=dim)
        done.append(dim)
    return x


def advance(padded, inner_uptake, diffuse, decays):
    center = padded[:, 1:-1, 1:-1, :]
    laplace = padded[:, 2:, 1:-1, :] + padded[:, :-2, 1:-1, :]
    laplace = laplace + padded[:, 1:-1, 2:, :] + padded[:, 1:-1, :-2, :]
    laplace = laplace + jnp.roll(center, -1, 3) + jnp.roll(center, 1, 3)
    laplace = laplace - 6.0 * center
    return center + diffuse * laplace - decays * inner_uptake[None] * center


def local(substrates, uptake, diffusion, decay_rate):
    diffuse = diffusion[:, None, None, None]
    decays = decay_rate[:, None, None, None]
    concentration = substrates
    for substep in range(SUBSTEPS):
        padded = extended(concentration, (("gx", 1), ("gy", 2)), 1)
        concentration = advance(padded, uptake, diffuse, decays)
    return concentration


def solution(mesh):
    placed = (P(None, "gx", "gy", None), P("gx", "gy", None), P(), P())
    return jax.shard_map(
        local, mesh=mesh, in_specs=placed, out_specs=P(None, "gx", "gy", None), check_vma=False
    )
```

profile of v0, /device:TPU:0, one launch (start us, length us, event | category | flops | bytes accessed | tf_op | source)
XLA Modules:
  0.0 101.3 jit_solution(14884354842010058708)
XLA Ops:
  0.0 0.9 fusion.59
  0.9 4.2 %collective-permute-start = (f32[8,1,16,128]{3,1,2,0:T(1,128)S(1)}, f32[8,1,16,128]{3,1,2,0:T(1,128)S(1)}, u32[]{:S(2)}, u32[]{:S(2)}) collective-permute-start(f32[8,1,16,128]{3,1,2,0:T(1,128)S(1)} %bitcast.3), channel_id=1, source_target_pairs={{32,0},{64,32},{96,64},{128,96},{160,128},{192,160},{224,192},{0,2... | collective-permute-start | bytes 196616 | tf_op jit(solution)/shard_map/ppermute | solution.py:18
  5.1 3.4 %copy.17 = f32[8,64,16,128]{3,1,2,0:T(8,128)S(1)} copy(f32[8,64,16,128]{3,2,1,0:T(8,128)} %param.4) | data formatting | bytes 8388608 | tf_op args[0]
  8.6 4.4 %collective-permute-start.2 = (f32[8,64,1,128]{3,1,2,0:T(8,128)S(1)}, f32[8,64,1,128]{3,1,2,0:T(8,128)S(1)}, u32[]{:S(2)}, u32[]{:S(2)}) collective-permute-start(f32[8,64,1,128]{3,1,2,0:T(8,128)S(1)} %get-tuple-element.33), channel_id=1, source_target_pairs={{1,0},{2,1},{3,2},{4,3},{5,4},{6,5},{7,6},{8,7},{9,8},{10,9},{11,1... | collective-permute-start | bytes 786440 | tf_op jit(solution)/shard_map/ppermute | solution.py:18
  13.1 1.7 %fusion.57 = (f32[8,64,16,127]{3,1,2,0:T(8,128)S(1)}, f32[8,64,16,127]{3,1,2,0:T(8,128)S(1)}) fusion(f32[8,64,16,128]{3,1,2,0:T(8,128)S(1)} %copy.17), kind=kLoop, calls=%fused_computation.95 | loop fusion | bytes 16646144 | tf_op jit(solution)/shard_map/jit(_roll_static)/slice | solution.py:33
  14.7 0.0 copy-start
  14.7 0.0 copy-start.1
  14.7 0.0 copy-start.2
  14.8 3.4 %fusion.56 = (f32[8,64,16,1]{3,1,2,0:T(8,128)S(1)}, f32[8,64,16,1]{3,1,2,0:T(8,128)}) fusion(f32[8,64,16,128]{3,1,2,0:T(8,128)S(1)} %copy.17), kind=kLoop, calls=%fused_computation.94 | loop fusion | bytes 131072 | tf_op jit(solution)/shard_map/jit(_roll_static)/slice | solution.py:33
  18.2 0.2 copy.18
  18.4 0.0 collective-permute-done
  18.4 0.0 collective-permute-done.2
  18.4 3.8 %collective-permute-done.3 = f32[8,64,1,128]{3,1,2,0:T(8,128)S(1)} collective-permute-done((f32[8,64,1,128]{3,1,2,0:T(8,128)S(1)}, f32[8,64,1,128]{3,1,2,0:T(8,128)S(1)}, u32[]{:S(2)}, u32[]{:S(2)}) %collective-permute-start.3) | collective-permute-done | bytes 262176 | tf_op jit(solution)/shard_map/ppermute | solution.py:17
  22.2 7.5 %fusion = f32[8,64,16,128]{3,1,2,0:T(8,128)S(1)} fusion(f32[8,64,16,128]{3,1,2,0:T(8,128)S(1)} %copy.17, f32[8,64,1,128]{3,1,2,0:T(8,128)S(1)} %collective-permute-done.3, f32[8,1,16,128]{3,1,2,0:T(1,128)S(1)} %collective-permute-done, f32[8,1,16,128]{3,1,2,0:T(1,128)S(1)} %collective-permute-done.1, f32[8,64,1,128]{3,1,2,0:T(8,128)S(1)} %collective-permute-done.2, ...), kind=kLoop, calls=%fused_computation.4 | loop fusion | flops 29360128 | bytes 17956928 | tf_op jit(solution)/shard_map/sub | solution.py:35
  29.6 0.1 fusion.55
  29.8 1.7 %fusion.52 = (f32[8,64,16,1]{3,1,2,0:T(8,128)S(1)}, f32[8,64,16,1]{3,1,2,0:T(8,128)S(1)}) fusion(f32[8,64,16,128]{3,1,2,0:T(8,128)S(1)} %fusion), kind=kLoop, calls=%fused_computation.90 | loop fusion | bytes 131072 | tf_op jit(solution)/shard_map/jit(_roll_static)/slice | solution.py:33
  31.5 0.1 collective-permute-start.5
  31.6 3.2 %collective-permute-start.4 = (f32[8,1,16,128]{3,1,2,0:T(1,128)S(1)}, f32[8,1,16,128]{3,1,2,0:T(1,128)S(1)}, u32[]{:S(2)}, u32[]{:S(2)}) collective-permute-start(f32[8,1,16,128]{3,1,2,0:T(1,128)S(1)} %get-tuple-element.28), channel_id=1, source_target_pairs={{32,0},{64,32},{96,64},{128,96},{160,128},{192,160},{224,192},{0,2... | collective-permute-start | bytes 196616 | tf_op jit(solution)/shard_map/ppermute | solution.py:18
  34.8 1.0 %collective-permute-start.6 = (f32[8,64,1,128]{3,1,2,0:T(8,128)S(1)}, f32[8,64,1,128]{3,1,2,0:T(8,128)S(1)}, u32[]{:S(2)}, u32[]{:S(2)}) collective-permute-start(f32[8,64,1,128]{3,1,2,0:T(8,128)S(1)} %get-tuple-element.25), channel_id=1, source_target_pairs={{1,0},{2,1},{3,2},{4,3},{5,4},{6,5},{7,6},{8,7},{9,8},{10,9},{11,1... | collective-permute-start | bytes 786440 | tf_op jit(solution)/shard_map/ppermute | solution.py:18
  35.8 3.7 %fusion.53 = (f32[8,64,16,127]{3,1,2,0:T(8,128)S(1)}, f32[8,64,16,127]{3,1,2,0:T(8,128)}) fusion(f32[8,64,16,128]{3,1,2,0:T(8,128)S(1)} %fusion), kind=kLoop, calls=%fused_computation.91 | loop fusion | bytes 16646144 | tf_op jit(solution)/shard_map/jit(_roll_static)/slice | solution.py:33
  39.5 0.0 collective-permute-done.4
  39.5 0.2 collective-permute-done.6
  39.7 5.2 %collective-permute-done.7 = f32[8,64,1,128]{3,1,2,0:T(8,128)S(1)} collective-permute-done((f32[8,64,1,128]{3,1,2,0:T(8,128)S(1)}, f32[8,64,1,128]{3,1,2,0:T(8,128)S(1)}, u32[]{:S(2)}, u32[]{:S(2)}) %collective-permute-start.7) | collective-permute-done | bytes 262176 | tf_op jit(solution)/shard_map/ppermute | solution.py:17
  44.9 7.8 %fusion.1 = f32[8,64,16,128]{3,1,2,0:T(8,128)S(1)} fusion(f32[8,64,16,128]{3,1,2,0:T(8,128)S(1)} %fusion, f32[8,64,1,128]{3,1,2,0:T(8,128)S(1)} %collective-permute-done.7, f32[8,1,16,128]{3,1,2,0:T(1,128)S(1)} %collective-permute-done.4, f32[8,1,16,128]{3,1,2,0:T(1,128)S(1)} %collective-permute-done.5, f32[8,64,1,128]{3,1,2,0:T(8,128)S(1)} %collective-permute-done.6, ...), kind=kLoop, calls=%fused_computation.5 | loop fusion | flops 29360128 | bytes 17956928 | tf_op jit(solution)/shard_map/sub | solution.py:35
  52.7 0.1 fusion.51
  52.8 1.7 %fusion.48 = (f32[8,64,16,1]{3,1,2,0:T(8,128)S(1)}, f32[8,64,16,1]{3,1,2,0:T(8,128)S(1)}) fusion(f32[8,64,16,128]{3,1,2,0:T(8,128)S(1)} %fusion.1), kind=kLoop, calls=%fused_computation.86 | loop fusion | bytes 131072 | tf_op jit(solution)/shard_map/jit(_roll_static)/slice | solution.py:33
  54.5 0.1 collective-permute-start.9
  54.6 3.2 %collective-permute-start.8 = (f32[8,1,16,128]{3,1,2,0:T(1,128)S(1)}, f32[8,1,16,128]{3,1,2,0:T(1,128)S(1)}, u32[]{:S(2)}, u32[]{:S(2)}) collective-permute-start(f32[8,1,16,128]{3,1,2,0:T(1,128)S(1)} %get-tuple-element.20), channel_id=1, source_target_pairs={{32,0},{64,32},{96,64},{128,96},{160,128},{192,160},{224,192},{0,2... | collective-permute-start | bytes 196616 | tf_op jit(solution)/shard_map/ppermute | solution.py:18
  57.8 0.0 collective-permute-start.10
  57.8 0.5 collective-permute-start.11
  58.3 3.7 %fusion.49 = (f32[8,64,16,127]{3,1,2,0:T(8,128)S(1)}, f32[8,64,16,127]{3,1,2,0:T(8,128)}) fusion(f32[8,64,16,128]{3,1,2,0:T(8,128)S(1)} %fusion.1), kind=kLoop, calls=%fused_computation.87 | loop fusion | bytes 16646144 | tf_op jit(solution)/shard_map/jit(_roll_static)/slice | solution.py:33
  62.0 0.0 collective-permute-done.9
  62.0 0.0 collective-permute-done.8
  62.0 4.9 %collective-permute-done.11 = f32[8,64,1,128]{3,1,2,0:T(8,128)S(1)} collective-permute-done((f32[8,64,1,128]{3,1,2,0:T(8,128)S(1)}, f32[8,64,1,128]{3,1,2,0:T(8,128)S(1)}, u32[]{:S(2)}, u32[]{:S(2)}) %collective-permute-start.11) | collective-permute-done | bytes 262176 | tf_op jit(solution)/shard_map/ppermute | solution.py:17
  66.9 7.8 %fusion.2 = f32[8,64,16,128]{3,1,2,0:T(8,128)S(1)} fusion(f32[8,64,16,128]{3,1,2,0:T(8,128)S(1)} %fusion.1, f32[8,64,1,128]{3,1,2,0:T(8,128)S(1)} %collective-permute-done.11, f32[8,1,16,128]{3,1,2,0:T(1,128)S(1)} %collective-permute-done.8, f32[8,1,16,128]{3,1,2,0:T(1,128)S(1)} %collective-permute-done.9, f32[8,64,1,128]{3,1,2,0:T(8,128)S(1)} %collective-permute-done.10, ...), kind=kLoop, calls=%fused_computation.6 | loop fusion | flops 29360128 | bytes 17956928 | tf_op jit(solution)/shard_map/sub | solution.py:35
  74.7 0.7 fusion.47
  75.5 1.7 %fusion.44 = (f32[8,64,16,1]{3,1,2,0:T(8,128)S(1)}, f32[8,64,16,1]{3,1,2,0:T(8,128)S(1)}) fusion(f32[8,64,16,128]{3,1,2,0:T(8,128)S(1)} %fusion.2), kind=kLoop, calls=%fused_computation.82 | loop fusion | bytes 131072 | tf_op jit(solution)/shard_map/jit(_roll_static)/slice | solution.py:33
  77.2 0.1 collective-permute-start.13
  77.3 3.2 %collective-permute-start.12 = (f32[8,1,16,128]{3,1,2,0:T(1,128)}, f32[8,1,16,128]{3,1,2,0:T(1,128)}, u32[]{:S(2)}, u32[]{:S(2)}) collective-permute-start(f32[8,1,16,128]{3,1,2,0:T(1,128)} %get-tuple-element.12), channel_id=1, source_target_pairs={{32,0},{64,32},{96,64},{128,96},{160,128},{192,160},{224,192},{0,2... | collective-permute-start | bytes 196616 | tf_op jit(solution)/shard_map/ppermute | solution.py:18
  80.5 0.0 collective-permute-start.14
  80.5 0.5 collective-permute-start.15
  81.0 1.7 %fusion.45 = (f32[8,64,16,127]{3,1,2,0:T(8,128)S(1)}, f32[8,64,16,127]{3,1,2,0:T(8,128)S(1)}) fusion(f32[8,64,16,128]{3,1,2,0:T(8,128)S(1)} %fusion.2), kind=kLoop, calls=%fused_computation.83 | loop fusion | bytes 16646144 | tf_op jit(solution)/shard_map/jit(_roll_static)/slice | solution.py:33
  82.7 0.4 collective-permute-done.13
  83.0 0.0 collective-permute-done.12
  83.0 1.3 %collective-permute-done.14 = f32[8,64,1,128]{3,1,2,0:T(8,128)S(1)} collective-permute-done((f32[8,64,1,128]{3,1,2,0:T(8,128)S(1)}, f32[8,64,1,128]{3,1,2,0:T(8,128)S(1)}, u32[]{:S(2)}, u32[]{:S(2)}) %collective-permute-start.14) | collective-permute-done | bytes 262176 | tf_op jit(solution)/shard_map/ppermute | solution.py:18
  84.4 5.2 %collective-permute-done.15 = f32[8,64,1,128]{3,1,2,0:T(8,128)S(1)} collective-permute-done((f32[8,64,1,128]{3,1,2,0:T(8,128)S(1)}, f32[8,64,1,128]{3,1,2,0:T(8,128)S(1)}, u32[]{:S(2)}, u32[]{:S(2)}) %collective-permute-start.15) | collective-permute-done | bytes 262176 | tf_op jit(solution)/shard_map/ppermute | solution.py:17
  89.6 7.3 %fusion.3 = f32[8,64,16,128]{3,1,2,0:T(8,128)S(1)} fusion(f32[8,64,16,128]{3,1,2,0:T(8,128)S(1)} %fusion.2, f32[8,64,1,128]{3,1,2,0:T(8,128)S(1)} %collective-permute-done.15, f32[8,1,16,128]{3,1,2,0:T(1,128)} %collective-permute-done.12, f32[8,1,16,128]{3,1,2,0:T(1,128)} %collective-permute-done.13, f32[8,64,1,128]{3,1,2,0:T(8,128)S(1)} %collective-permute-done.14, ...), kind=kLoop, calls=%fused_computation.7 | loop fusion | flops 29360128 | bytes 17956928 | tf_op jit(solution)/shard_map/sub | solution.py:35
  96.9 4.4 %copy.20 = f32[8,64,16,128]{3,2,1,0:T(8,128)} copy(f32[8,64,16,128]{3,1,2,0:T(8,128)S(1)} %fusion.3) | data formatting | bytes 8388608 | tf_op jit(solution)/shard_map/sub | solution.py:35
  (13 shorter events, 0.2 us)
Async XLA Ops:
  0.9 17.5 %collective-permute-start = (f32[8,1,16,128]{3,1,2,0:T(1,128)S(1)}, f32[8,1,16,128]{3,1,2,0:T(1,128)S(1)}, u32[]{:S(2)}, u32[]{:S(2)}) collective-permute-start(f32[8,1,16,128]{3,1,2,0:T(1,128)S(1)} %bitcast.3), channel_id=1, source_target_pairs={{32,0},{64,32},{96,64},{128,96},{160,128},{192,160},{224,192},{0,2... | collective-permute-start | bytes 196616 | tf_op jit(solution)/shard_map/ppermute | solution.py:18
  5.1 13.3 %collective-permute-start.1 = (f32[8,1,16,128]{3,1,2,0:T(1,128)S(1)}, f32[8,1,16,128]{3,1,2,0:T(1,128)S(1)}, u32[]{:S(2)}, u32[]{:S(2)}) collective-permute-start(f32[8,1,16,128]{3,1,2,0:T(1,128)S(1)} %bitcast.2), channel_id=1, source_target_pairs={{0,32},{32,64},{64,96},{96,128},{128,160},{160,192},{192,224},{224... | collective-permute-start | bytes 196616 | tf_op jit(solution)/shard_map/ppermute | solution.py:17
  8.6 9.8 %collective-permute-start.2 = (f32[8,64,1,128]{3,1,2,0:T(8,128)S(1)}, f32[8,64,1,128]{3,1,2,0:T(8,128)S(1)}, u32[]{:S(2)}, u32[]{:S(2)}) collective-permute-start(f32[8,64,1,128]{3,1,2,0:T(8,128)S(1)} %get-tuple-element.33), channel_id=1, source_target_pairs={{1,0},{2,1},{3,2},{4,3},{5,4},{6,5},{7,6},{8,7},{9,8},{10,9},{11,1... | collective-permute-start | bytes 786440 | tf_op jit(solution)/shard_map/ppermute | solution.py:18
  13.1 9.1 %collective-permute-start.3 = (f32[8,64,1,128]{3,1,2,0:T(8,128)S(1)}, f32[8,64,1,128]{3,1,2,0:T(8,128)S(1)}, u32[]{:S(2)}, u32[]{:S(2)}) collective-permute-start(f32[8,64,1,128]{3,1,2,0:T(8,128)S(1)} %get-tuple-element.34), channel_id=1, source_target_pairs={{0,1},{1,2},{2,3},{3,4},{4,5},{5,6},{6,7},{7,8},{8,9},{9,10},{10,1... | collective-permute-start | bytes 786440 | tf_op jit(solution)/shard_map/ppermute | solution.py:17
  14.7 3.5 %copy-start = (f32[64,16,128]{2,1,0:T(8,128)S(1)}, f32[64,16,128]{2,1,0:T(8,128)}, u32[]{:S(2)}) copy-start(f32[64,16,128]{2,1,0:T(8,128)} %param.5) | copy-start | bytes 1572868
  14.7 7.4 %copy-start.1 = (f32[8]{0:T(128)S(1)}, f32[8]{0:T(128)}, u32[]{:S(2)}) copy-start(f32[8]{0:T(128)} %param.7) | copy-start | bytes 100
  14.7 7.4 %copy-start.2 = (f32[8]{0:T(128)S(1)}, f32[8]{0:T(128)}, u32[]{:S(2)}) copy-start(f32[8]{0:T(128)} %param.6) | copy-start | bytes 100
  31.5 8.1 %collective-permute-start.5 = (f32[8,1,16,128]{3,1,2,0:T(1,128)S(1)}, f32[8,1,16,128]{3,1,2,0:T(1,128)S(1)}, u32[]{:S(2)}, u32[]{:S(2)}) collective-permute-start(f32[8,1,16,128]{3,1,2,0:T(1,128)S(1)} %get-tuple-element.27), channel_id=1, source_target_pairs={{0,32},{32,64},{64,96},{96,128},{128,160},{160,192},{192,224},{224... | collective-permute-start | bytes 196616 | tf_op jit(solution)/shard_map/ppermute | solution.py:17
  31.6 8.0 %collective-permute-start.4 = (f32[8,1,16,128]{3,1,2,0:T(1,128)S(1)}, f32[8,1,16,128]{3,1,2,0:T(1,128)S(1)}, u32[]{:S(2)}, u32[]{:S(2)}) collective-permute-start(f32[8,1,16,128]{3,1,2,0:T(1,128)S(1)} %get-tuple-element.28), channel_id=1, source_target_pairs={{32,0},{64,32},{96,64},{128,96},{160,128},{192,160},{224,192},{0,2... | collective-permute-start | bytes 196616 | tf_op jit(solution)/shard_map/ppermute | solution.py:18
  34.8 4.9 %collective-permute-start.6 = (f32[8,64,1,128]{3,1,2,0:T(8,128)S(1)}, f32[8,64,1,128]{3,1,2,0:T(8,128)S(1)}, u32[]{:S(2)}, u32[]{:S(2)}) collective-permute-start(f32[8,64,1,128]{3,1,2,0:T(8,128)S(1)} %get-tuple-element.25), channel_id=1, source_target_pairs={{1,0},{2,1},{3,2},{4,3},{5,4},{6,5},{7,6},{8,7},{9,8},{10,9},{11,1... | collective-permute-start | bytes 786440 | tf_op jit(solution)/shard_map/ppermute | solution.py:18
  35.8 9.1 %collective-permute-start.7 = (f32[8,64,1,128]{3,1,2,0:T(8,128)S(1)}, f32[8,64,1,128]{3,1,2,0:T(8,128)S(1)}, u32[]{:S(2)}, u32[]{:S(2)}) collective-permute-start(f32[8,64,1,128]{3,1,2,0:T(8,128)S(1)} %get-tuple-element.26), channel_id=1, source_target_pairs={{0,1},{1,2},{2,3},{3,4},{4,5},{5,6},{6,7},{7,8},{8,9},{9,10},{10,1... | collective-permute-start | bytes 786440 | tf_op jit(solution)/shard_map/ppermute | solution.py:17
  54.5 7.5 %collective-permute-start.9 = (f32[8,1,16,128]{3,1,2,0:T(1,128)S(1)}, f32[8,1,16,128]{3,1,2,0:T(1,128)S(1)}, u32[]{:S(2)}, u32[]{:S(2)}) collective-permute-start(f32[8,1,16,128]{3,1,2,0:T(1,128)S(1)} %get-tuple-element.19), channel_id=1, source_target_pairs={{0,32},{32,64},{64,96},{96,128},{128,160},{160,192},{192,224},{224... | collective-permute-start | bytes 196616 | tf_op jit(solution)/shard_map/ppermute | solution.py:17
  54.6 7.4 %collective-permute-start.8 = (f32[8,1,16,128]{3,1,2,0:T(1,128)S(1)}, f32[8,1,16,128]{3,1,2,0:T(1,128)S(1)}, u32[]{:S(2)}, u32[]{:S(2)}) collective-permute-start(f32[8,1,16,128]{3,1,2,0:T(1,128)S(1)} %get-tuple-element.20), channel_id=1, source_target_pairs={{32,0},{64,32},{96,64},{128,96},{160,128},{192,160},{224,192},{0,2... | collective-permute-start | bytes 196616 | tf_op jit(solution)/shard_map/ppermute | solution.py:18
  57.8 4.2 %collective-permute-start.10 = (f32[8,64,1,128]{3,1,2,0:T(8,128)S(1)}, f32[8,64,1,128]{3,1,2,0:T(8,128)S(1)}, u32[]{:S(2)}, u32[]{:S(2)}) collective-permute-start(f32[8,64,1,128]{3,1,2,0:T(8,128)S(1)} %get-tuple-element.17), channel_id=1, source_target_pairs={{1,0},{2,1},{3,2},{4,3},{5,4},{6,5},{7,6},{8,7},{9,8},{10,9},{11,1... | collective-permute-start | bytes 786440 | tf_op jit(solution)/shard_map/ppermute | solution.py:18
  57.8 9.1 %collective-permute-start.11 = (f32[8,64,1,128]{3,1,2,0:T(8,128)S(1)}, f32[8,64,1,128]{3,1,2,0:T(8,128)S(1)}, u32[]{:S(2)}, u32[]{:S(2)}) collective-permute-start(f32[8,64,1,128]{3,1,2,0:T(8,128)S(1)} %get-tuple-element.18), channel_id=1, source_target_pairs={{0,1},{1,2},{2,3},{3,4},{4,5},{5,6},{6,7},{7,8},{8,9},{9,10},{10,1... | collective-permute-start | bytes 786440 | tf_op jit(solution)/shard_map/ppermute | solution.py:17
  77.2 5.9 %collective-permute-start.13 = (f32[8,1,16,128]{3,1,2,0:T(1,128)}, f32[8,1,16,128]{3,1,2,0:T(1,128)}, u32[]{:S(2)}, u32[]{:S(2)}) collective-permute-start(f32[8,1,16,128]{3,1,2,0:T(1,128)} %get-tuple-element.11), channel_id=1, source_target_pairs={{0,32},{32,64},{64,96},{96,128},{128,160},{160,192},{192,224},{224... | collective-permute-start | bytes 196616 | tf_op jit(solution)/shard_map/ppermute | solution.py:17
  77.3 5.8 %collective-permute-start.12 = (f32[8,1,16,128]{3,1,2,0:T(1,128)}, f32[8,1,16,128]{3,1,2,0:T(1,128)}, u32[]{:S(2)}, u32[]{:S(2)}) collective-permute-start(f32[8,1,16,128]{3,1,2,0:T(1,128)} %get-tuple-element.12), channel_id=1, source_target_pairs={{32,0},{64,32},{96,64},{128,96},{160,128},{192,160},{224,192},{0,2... | collective-permute-start | bytes 196616 | tf_op jit(solution)/shard_map/ppermute | solution.py:18
  80.5 3.9 %collective-permute-start.14 = (f32[8,64,1,128]{3,1,2,0:T(8,128)S(1)}, f32[8,64,1,128]{3,1,2,0:T(8,128)S(1)}, u32[]{:S(2)}, u32[]{:S(2)}) collective-permute-start(f32[8,64,1,128]{3,1,2,0:T(8,128)S(1)} %get-tuple-element.9), channel_id=1, source_target_pairs={{1,0},{2,1},{3,2},{4,3},{5,4},{6,5},{7,6},{8,7},{9,8},{10,9},{11,1... | collective-permute-start | bytes 786440 | tf_op jit(solution)/shard_map/ppermute | solution.py:18
  80.5 9.1 %collective-permute-start.15 = (f32[8,64,1,128]{3,1,2,0:T(8,128)S(1)}, f32[8,64,1,128]{3,1,2,0:T(8,128)S(1)}, u32[]{:S(2)}, u32[]{:S(2)}) collective-permute-start(f32[8,64,1,128]{3,1,2,0:T(8,128)S(1)} %get-tuple-element.10), channel_id=1, source_target_pairs={{0,1},{1,2},{2,3},{3,4},{4,5},{5,6},{6,7},{7,8},{8,9},{9,10},{10,1... | collective-permute-start | bytes 786440 | tf_op jit(solution)/shard_map/ppermute | solution.py:17
where the time goes:
time: 102 us; the launch traced here: 101 us
  other arithmetic  30.3 us (30%)
  local copies, waits for them, and re-layouts  29.1 us (29%)
  waiting for transfers between devices  21.1 us (21%)
  starting transfers between devices  20.7 us (20%)
    sub x4, other arithmetic, advance(): return center + diffuse * laplace - decays * inner_uptake[None] * center  30.3 us
    ppermute x8, waiting for transfers between devices, extended(): lax.ppermute(last, axis, up)  19.5 us
    ppermute x8, starting transfers between devices, extended(): lax.ppermute(first, axis, [(b, a) for a, b in up])  19.4 us
    slice x8, local copies, waits for them, and re-layouts, advance(): laplace = laplace + jnp.roll(center, -1, 3) + jnp.roll(center, 1, 3)  19.1 us
    sub x1, local copies, waits for them, and re-layouts, advance(): return center + diffuse * laplace - decays * inner_uptake[None] * center  4.39 us
    unnamed x8, local copies, waits for them, and re-layouts  3.63 us
  transfers between devices with their start and end apart: 16, of which 7 were waited for; matrix products, arithmetic and copies ran while one was open for 18% of the time, Pallas kernels for 0%

commit v1 on v0

v1 whole, which is shorter than its diff:
```python
import functools

import jax
import jax.numpy as jnp
from jax import lax
from jax.experimental import pallas as pl
from jax.experimental.pallas import tpu as pltpu
from jax.sharding import PartitionSpec as P

S, CX, CY, CZ = 8, 64, 16, 128
W = 2
PX, PY = CX + 2 * W, CY + 2 * W
MESH = pl.DeviceIdType.MESH

FACES = ((0, 1), (0, -1), (1, 0), (-1, 0))
CORNERS = ((1, 1), (1, -1), (-1, 1), (-1, -1))


def sent(step, size, width, around):
    if step == 0:
        return pl.ds(around, size), pl.ds(around, size)
    if step > 0:
        return pl.ds(around + size - width, width), pl.ds(around - width, width)
    return pl.ds(around, width), pl.ds(around + size, width)


def substep(src, dst, up, rate, decay, planes, group, starts, up_at, dst_at):
    stay = 1.0 - 6.0 * rate

    def body(g, carry):
        for n in range(group):
            i = g * group + n
            for j in starts:
                center = src[i + 1, j + 1 : j + 9, :]
                total = src[i + 1, j : j + 8, :] + src[i + 1, j + 2 : j + 10, :]
                total = total + (src[i, j + 1 : j + 9, :] + src[i + 2, j + 1 : j + 9, :])
                total = total + (pltpu.roll(center, 1, 1) + pltpu.roll(center, CZ - 1, 1))
                keep = stay - decay * up[i + up_at, j + up_at : j + up_at + 8, :]
                dst[i + dst_at, j + dst_at : j + dst_at + 8, :] = keep * center + rate * total
        return carry

    lax.fori_loop(0, planes // group, body, 0)


def kernel(
    nx, ny, x_hbm, u_hbm, d_hbm, k_hbm, out, d_ref, k_ref,
    first, second, half, up, load_sem, send_sem, recv_sem, corner_send, corner_recv, up_send, up_recv,
):
    gx, gy = lax.axis_index("gx"), lax.axis_index("gy")

    def device(step):
        return (lax.rem(gx + step[0] + nx, nx), lax.rem(gy + step[1] + ny, ny))

    def load(s):
        return pltpu.make_async_copy(
            x_hbm.at[s], first.at[s, pl.ds(W, CX), pl.ds(W, CY)], load_sem.at[s]
        )

    load_up = pltpu.make_async_copy(
        u_hbm, up.at[pl.ds(1, CX), pl.ds(1, CY)], load_sem.at[S]
    )
    for s in range(S):
        load(s).start()
    load_up.start()
    load_d = pltpu.make_async_copy(d_hbm, d_ref, load_sem.at[S + 1])
    load_k = pltpu.make_async_copy(k_hbm, k_ref, load_sem.at[S + 2])
    load_d.start()
    load_k.start()

    barrier = pltpu.get_barrier_semaphore()
    for step in FACES + CORNERS:
        pl.semaphore_signal(barrier, inc=1, device_id=device(step), device_id_type=MESH)
    pl.semaphore_wait(barrier, len(FACES + CORNERS))

    def face(buffer, r, s, d):
        step = FACES[d]
        (x_from, x_to), (y_from, y_to) = sent(step[0], CX, W, W), sent(step[1], CY, W, W)
        return pltpu.make_async_remote_copy(
            src_ref=buffer.at[s, x_from, y_from], dst_ref=buffer.at[s, x_to, y_to],
            send_sem=send_sem.at[r, s, d], recv_sem=recv_sem.at[r, s, d],
            device_id=device(step), device_id_type=MESH,
        )

    def corner(buffer, which, slot, d):
        step = CORNERS[d]
        (x_from, x_to), (y_from, y_to) = sent(step[0], CX, 1, W), sent(step[1], CY, 1, W)
        return pltpu.make_async_remote_copy(
            src_ref=buffer.at[which, x_from, y_from], dst_ref=buffer.at[which, x_to, y_to],
            send_sem=corner_send.at[slot, d], recv_sem=corner_recv.at[slot, d],
            device_id=device(step), device_id_type=MESH,
        )

    def up_face(d):
        step = FACES[d]
        (x_from, x_to), (y_from, y_to) = sent(step[0], CX, 1, 1), sent(step[1], CY, 1, 1)
        return pltpu.make_async_remote_copy(
            src_ref=up.at[x_from, y_from], dst_ref=up.at[x_to, y_to],
            send_sem=up_send.at[d], recv_sem=up_recv.at[d],
            device_id=device(step), device_id_type=MESH,
        )

    for s in range(S):
        load(s).wait()
    load_up.wait()
    load_d.wait()
    load_k.wait()
    whole = pl.ds(0, S)
    for d in range(4):
        face(first, 0, 0, d).start()
    for d in range(4):
        up_face(d).start()
    for d in range(4):
        corner(first, whole, S, d).start()

    def send(s, carry):
        for d in range(4):
            face(first, 0, s, d).start()
        return carry

    lax.fori_loop(1, S, send, 0)

    for d in range(4):
        up_face(d).wait_recv()
    for d in range(4):
        corner(first, whole, S, d).wait_recv()

    outer = (0, 8, CY + 2 - 8)
    inner = (0, 8)

    def advance(buffer, s, result, at):
        rate, decay = d_ref[s], k_ref[s]
        substep(buffer.at[s], half, up, rate, decay, CX + 2, 6, outer, 0, 0)
        substep(half, result.at[s], up, rate, decay, CX, 8, inner, 1, at)

    def round_one(s, carry):
        for d in range(4):
            face(first, 0, s, d).wait_recv()
        advance(first, s, second, W)
        for d in range(4):
            corner(second, pl.ds(s, 1), s, d).start()
        for d in range(4):
            face(second, 1, s, d).start()
        return carry

    lax.fori_loop(0, S, round_one, 0)

    def round_two(s, carry):
        for d in range(4):
            face(second, 1, s, d).wait_recv()
        for d in range(4):
            corner(second, pl.ds(s, 1), s, d).wait_recv()
        advance(second, s, out, 0)
        return carry

    lax.fori_loop(0, S, round_two, 0)

    def drain(s, carry):
        for d in range(4):
            face(first, 0, s, d).wait_send()
            face(second, 1, s, d).wait_send()
            corner(second, pl.ds(s, 1), s, d).wait_send()
        return carry

    lax.fori_loop(0, S, drain, 0)
    for d in range(4):
        up_face(d).wait_send()
        corner(first, whole, S, d).wait_send()


def solution(mesh):
    nx, ny = mesh.shape["gx"], mesh.shape["gy"]

    def local(*arrays):
        arrays = [pltpu.with_memory_space_constraint(a, pltpu.HBM) for a in arrays]
        return pl.pallas_call(
            functools.partial(kernel, nx, ny),
            out_shape=jax.ShapeDtypeStruct((S, CX, CY, CZ), jnp.float32),
            in_specs=[pl.BlockSpec(memory_space=pltpu.HBM)] * 4,
            out_specs=pl.BlockSpec(memory_space=pltpu.VMEM),
            scratch_shapes=[
                pltpu.SMEM((S,), jnp.float32),
                pltpu.SMEM((S,), jnp.float32),
                pltpu.VMEM((S, PX, PY, CZ), jnp.float32),
                pltpu.VMEM((S, PX, PY, CZ), jnp.float32),
                pltpu.VMEM((CX + 2, CY + 2, CZ), jnp.float32),
                pltpu.VMEM((CX + 2, CY + 2, CZ), jnp.float32),
                pltpu.SemaphoreType.DMA((S + 3,)),
                pltpu.SemaphoreType.DMA((2, S, 4)),
                pltpu.SemaphoreType.DMA((2, S, 4)),
                pltpu.SemaphoreType.DMA((S + 1, 4)),
                pltpu.SemaphoreType.DMA((S + 1, 4)),
                pltpu.SemaphoreType.DMA((4,)),
                pltpu.SemaphoreType.DMA((4,)),
            ],
            compiler_params=pltpu.CompilerParams(
                collective_id=0, has_side_effects=True, vmem_limit_bytes=40 << 20
            ),
        )(*arrays)

    placed = (P(None, "gx", "gy", None), P("gx", "gy", None), P(), P())
    return jax.shard_map(
        local, mesh=mesh, in_specs=placed, out_specs=P(None, "gx", "gy", None), check_vma=False
    )
```

time: 102 us -> 51.9 us (0.51)
  the two profiles are of different devices: /device:TPU:0 before, /device:TPU:1 now
where the time goes in v1:
time: 51.9 us; the launch traced here: 51.8 us
  Pallas kernels  49.8 us (96%)
  local copies, waits for them, and re-layouts  2.02 us (4%)
    pallas_call x1, Pallas kernels, local(): pl.pallas_call(functools.partial(kernel, nx, ny), out_shape=jax.ShapeDtyp...  49.8 us
    unnamed x1, local copies, waits for them, and re-layouts  2.02 us

profile of v1, /device:TPU:1, one launch (start us, length us, event | category | flops | bytes accessed | tf_op | source)
XLA Modules:
  0.0 51.8 jit_solution(713939537879350848)
XLA Ops:
  0.0 49.8 %shard_map.46 = f32[8,64,16,128]{3,2,1,0:T(8,128)S(1)} custom-call(f32[8,64,16,128]{3,2,1,0:T(8,128)} %x_hbm.1, f32[64,16,128]{2,1,0:T(8,128)} %u_hbm.1, f32[8]{0:T(128)} %d_hbm.1, f32[8]{0:T(128)} %k_hbm.1), custom_call_target="tpu_custom_call" | custom-call | tf_op jit(solution)/shard_map/pallas_call | solution.py:175
  49.8 2.0 %copy.6 = f32[8,64,16,128]{3,2,1,0:T(8,128)} copy(f32[8,64,16,128]{3,2,1,0:T(8,128)S(1)} %shard_map.46) | data formatting | bytes 8388608

commit v2 on v1

--- a/solution.py
+++ b/solution.py
@@ -24,22 +24,27 @@
     return pl.ds(around, width), pl.ds(around + size, width)
 
 
-def substep(src, dst, up, rate, decay, planes, group, starts, up_at, dst_at):
+def neighbours_in_z(z_sum, center, by_matmul):
+    cells = center[:by_matmul].reshape(by_matmul * 8, CZ)
+    high = cells.astype(jnp.bfloat16)
+    low = (cells - high.astype(jnp.float32)).astype(jnp.bfloat16)
+    first = jnp.dot(
+        jnp.concatenate([high, low], axis=1), z_sum, preferred_element_type=jnp.float32
+    ).reshape(by_matmul, 8, CZ)
+    rest = center[by_matmul:]
+    return jnp.concatenate([first, pltpu.roll(rest, 1, 2) + pltpu.roll(rest, CZ - 1, 2)], axis=0)
+
+
+def substep(src, dst, up, z_sum, rate, decay, planes, starts, up_at, dst_at):
     stay = 1.0 - 6.0 * rate
-
-    def body(g, carry):
-        for n in range(group):
-            i = g * group + n
-            for j in starts:
-                center = src[i + 1, j + 1 : j + 9, :]
-                total = src[i + 1, j : j + 8, :] + src[i + 1, j + 2 : j + 10, :]
-                total = total + (src[i, j + 1 : j + 9, :] + src[i + 2, j + 1 : j + 9, :])
-                total = total + (pltpu.roll(center, 1, 1) + pltpu.roll(center, CZ - 1, 1))
-                keep = stay - decay * up[i + up_at, j + up_at : j + up_at + 8, :]
-                dst[i + dst_at, j + dst_at : j + dst_at + 8, :] = keep * center + rate * total
-        return carry
-
-    lax.fori_loop(0, planes // group, body, 0)
+    by_matmul = planes * 2 // 3
+    for j in starts:
+        center = src[1 : planes + 1, j + 1 : j + 9, :]
+        total = neighbours_in_z(z_sum, center, by_matmul)
+        total = total + (src[1 : planes + 1, j : j + 8, :] + src[1 : planes + 1, j + 2 : j + 10, :])
+        total = total + (src[0:planes, j + 1 : j + 9, :] + src[2 : planes + 2, j + 1 : j + 9, :])
+        keep = stay - decay * up[up_at : planes + up_at, j + up_at : j + up_at + 8, :]
+        dst[dst_at : planes + dst_at, j + dst_at : j + dst_at + 8, :] = keep * center + rate * total
 
 
 def kernel(
@@ -124,13 +129,18 @@
     for d in range(4):
         corner(first, whole, S, d).wait_recv()
 
+    apart = lax.rem(
+        lax.broadcasted_iota(jnp.int32, (2 * CZ, CZ), 0) - lax.broadcasted_iota(jnp.int32, (2 * CZ, CZ), 1) + CZ, CZ
+    )
+    z_sum = jnp.where((apart == 1) | (apart == CZ - 1), 1.0, 0.0).astype(jnp.bfloat16)
+
     outer = (0, 8, CY + 2 - 8)
     inner = (0, 8)
 
     def advance(buffer, s, result, at):
         rate, decay = d_ref[s], k_ref[s]
-        substep(buffer.at[s], half, up, rate, decay, CX + 2, 6, outer, 0, 0)
-        substep(half, result.at[s], up, rate, decay, CX, 8, inner, 1, at)
+        substep(buffer.at[s], half, up, z_sum, rate, decay, CX + 2, outer, 0, 0)
+        substep(half, result.at[s], up, z_sum, rate, decay, CX, inner, 1, at)
 
     def round_one(s, carry):
         for d in range(4):

time: 51.9 us -> 29.8 us (0.57)
  Pallas kernels: 49.8 us -> 27.7 us
    pallas_call x1, Pallas kernels: 49.8 us -> 27.7 us  [local(): pl.pallas_call(functools.partial(kernel, nx, ny), out_shape=jax.ShapeDtyp...]
where the time goes in v2:
time: 29.8 us; the launch traced here: 29.7 us
  Pallas kernels  27.7 us (93%)
  local copies, waits for them, and re-layouts  2.02 us (7%)
    pallas_call x1, Pallas kernels, local(): pl.pallas_call(functools.partial(kernel, nx, ny), out_shape=jax.ShapeDtyp...  27.7 us
    unnamed x1, local copies, waits for them, and re-layouts  2.02 us

profile of v2, /device:TPU:1, one launch (start us, length us, event | category | flops | bytes accessed | tf_op | source)
XLA Modules:
  0.0 29.7 jit_solution(9399452202376466106)
XLA Ops:
  0.0 27.7 %shard_map.46 = f32[8,64,16,128]{3,2,1,0:T(8,128)S(1)} custom-call(f32[8,64,16,128]{3,2,1,0:T(8,128)} %x_hbm.1, f32[64,16,128]{2,1,0:T(8,128)} %u_hbm.1, f32[8]{0:T(128)} %d_hbm.1, f32[8]{0:T(128)} %k_hbm.1), custom_call_target="tpu_custom_call" | custom-call | tf_op jit(solution)/shard_map/pallas_call | solution.py:185
  27.7 2.0 %copy.6 = f32[8,64,16,128]{3,2,1,0:T(8,128)} copy(f32[8,64,16,128]{3,2,1,0:T(8,128)S(1)} %shard_map.46) | data formatting | bytes 8388608

commit v3 on v0

v3 whole, which is shorter than its diff:
```python
import functools

import jax
import jax.numpy as jnp
from jax import lax
from jax.experimental import pallas as pl
from jax.experimental.pallas import tpu as pltpu
from jax.sharding import PartitionSpec as P

S, CX, CY, CZ = 8, 64, 16, 128
MESH = pl.DeviceIdType.MESH
PASS_ON, PASS_ON_FIRST, SEND_FIRST, BEFORE_EDGES = 1, 7, 2, 2

FIRST, SECOND, HALF, UP = (4, 2), (2, 2), (3, 1), (3, 1)
OUTER, INNER = (-1, 7, 9), (0, 8)


def neighbours_in_z(z_sum, center):
    by_matmul = center.shape[0] * 2 // 3
    cells = center[:by_matmul].reshape(by_matmul * 8, CZ)
    high = cells.astype(jnp.bfloat16)
    low = (cells - high.astype(jnp.float32)).astype(jnp.bfloat16)
    first = jnp.dot(
        jnp.concatenate([high, low], axis=1), z_sum, preferred_element_type=jnp.float32
    ).reshape(by_matmul, 8, CZ)
    rest = center[by_matmul:]
    return jnp.concatenate([first, pltpu.roll(rest, 1, 2) + pltpu.roll(rest, CZ - 1, 2)], axis=0)


def substep(jobs, up, z_sum):
    def at(ref, where, x, n, y):
        return ref.at[pl.ds(x + where[0], n), pl.ds(y + where[1], 8)]

    centers = [at(src, where, x, n, y)[...] for src, where, _, _, x, n, y, _, _ in jobs]
    sums, done = neighbours_in_z(z_sum, jnp.concatenate(centers, axis=0)), 0
    for center, (src, where, dst, to, x, n, y, rate, decay) in zip(centers, jobs, strict=True):
        total = sums[done : done + n]
        done += n
        total = total + (at(src, where, x, n, y - 1)[...] + at(src, where, x, n, y + 1)[...])
        total = total + (at(src, where, x - 1, n, y)[...] + at(src, where, x + 1, n, y)[...])
        keep = (1.0 - 6.0 * rate) - decay * at(up, UP, x, n, y)[...]
        at(dst, to, x, n, y)[...] = keep * center + rate * total


def kernel(
    nx, ny, x_hbm, u_hbm, d_hbm, k_hbm, out, d_ref, k_ref, first, second, half, edge, up,
    load_sem, y_send, y_recv, x_send, x_recv, up_send, up_recv, corner_send, corner_recv, above, below,
):
    gx, gy = lax.axis_index("gx"), lax.axis_index("gy")

    def device(dx, dy):
        return (lax.rem(gx + dx + nx, nx), lax.rem(gy + dy + ny, ny))

    def load(s):
        return pltpu.make_async_copy(x_hbm.at[s], first.at[s, pl.ds(4, CX), pl.ds(2, CY)], load_sem.at[s])

    load_up = pltpu.make_async_copy(u_hbm, up.at[pl.ds(3, CX), pl.ds(1, CY)], load_sem.at[S])
    load_d = pltpu.make_async_copy(d_hbm, d_ref, load_sem.at[S + 1])
    load_k = pltpu.make_async_copy(k_hbm, k_ref, load_sem.at[S + 2])

    is_first, is_last = gx == 0, gx == nx - 1
    barrier = pltpu.get_barrier_semaphore()

    def signal(sem, dx, dy):
        pl.semaphore_signal(sem, inc=1, device_id=device(dx, dy), device_id_type=MESH)

    signal(barrier, 0, 1)
    signal(barrier, 0, -1)
    pl.when(jnp.logical_not(is_last))(lambda: signal(barrier, 1, 0))
    pl.when(is_first)(lambda: signal(barrier, -1, 0))
    for s in range(S):
        load(s).start()
    for copy in (load_up, load_d, load_k):
        copy.start()

    def remote(src, dst, send_sem, recv_sem, to):
        return pltpu.make_async_remote_copy(
            src_ref=src, dst_ref=dst, send_sem=send_sem, recv_sem=recv_sem,
            device_id=to, device_id_type=MESH,
        )

    both = (0, 1)
    pairs = ((0, 0), (0, 1), (1, 0), (1, 1))
    rows = ((16, 0), (2, 18))
    all_s = pl.ds(0, S)

    def y_face(r, s, d):
        buffer, planes = ((first, pl.ds(4, CX)), (second, pl.ds(4, CX - 4)))[r]
        a, b = rows[d]
        return remote(
            buffer.at[s, planes, pl.ds(a, 2)], buffer.at[s, planes, pl.ds(b, 2)],
            y_send.at[r, d], y_recv.at[r, s, d], device(0, 1 - 2 * d),
        )

    def x_face(part, d):
        a, b = ((64, 0), (4, 68))[d]
        r = (pl.ds(2, 2), pl.ds(16, 2), pl.ds(4, 12))[part]
        return remote(
            first.at[all_s, pl.ds(a, 4), r], first.at[all_s, pl.ds(b, 4), r],
            x_send.at[d], x_recv.at[part, d], device(1 - 2 * d, 0),
        )

    def up_y(d):
        a, b = ((16, 0), (1, 17))[d]
        return remote(
            up.at[pl.ds(3, CX), pl.ds(a, 1)], up.at[pl.ds(3, CX), pl.ds(b, 1)],
            up_send.at[0, d], up_recv.at[0, d], device(0, 1 - 2 * d),
        )

    def up_x(d):
        a, b = ((64, 0), (3, 67))[d]
        return remote(
            up.at[pl.ds(a, 3), pl.ds(1, CY)], up.at[pl.ds(b, 3), pl.ds(1, CY)],
            up_send.at[1, d], up_recv.at[1, d], device(1 - 2 * d, 0),
        )

    def corner(kind, side, d):
        to = device(0, 1 - 2 * d)
        sems = corner_send.at[kind], corner_recv.at[kind]
        if kind == 0:
            planes, (a, b) = pl.ds((1, 68)[side], 3), rows[d]
            return remote(first.at[all_s, planes, pl.ds(a, 2)], first.at[all_s, planes, pl.ds(b, 2)], *sems, to)
        if kind == 1:
            planes, (a, b) = pl.ds((1, 67)[side], 2), ((16, 0), (1, 17))[d]
            return remote(up.at[planes, pl.ds(a, 1)], up.at[planes, pl.ds(b, 1)], *sems, to)
        planes, (a, b) = pl.ds((1, 64)[side], 3), rows[d]
        return remote(second.at[all_s, planes, pl.ds(a, 2)], second.at[all_s, planes, pl.ds(b, 2)], *sems, to)

    def corners_arrived(kind):
        ref = (first.at[all_s, pl.ds(0, 12), pl.ds(0, 2)], up.at[pl.ds(0, 8), pl.ds(0, 1)])[kind % 2]
        pltpu.make_async_copy(ref, ref, corner_recv.at[kind]).wait()

    pl.semaphore_wait(barrier, 2 + jnp.where(is_first, 0, 1) + jnp.where(is_last, 1, 0))
    pl.when(jnp.logical_not(is_first))(lambda: signal(above, -1, 0))
    pl.when(is_last)(lambda: signal(below, 1, 0))
    load(0).wait()
    for d in both:
        y_face(0, 0, d).start()
    load_up.wait()
    for d in both:
        up_y(d).start()
    for s in range(1, S):
        load(s).wait()
        for d in both:
            y_face(0, s, d).start()

    def send_along_gx(d):
        up_x(d).start()
        for part in range(3):
            x_face(part, d).start()

    pl.when(jnp.logical_not(is_first))(lambda: send_along_gx(1))
    pl.when(jnp.logical_not(is_last))(lambda: pl.semaphore_wait(above, 1))
    send_along_gx(0)
    load_d.wait()
    load_k.wait()

    apart = lax.rem(
        lax.broadcasted_iota(jnp.int32, (2 * CZ, CZ), 0) - lax.broadcasted_iota(jnp.int32, (2 * CZ, CZ), 1) + CZ, CZ
    )
    z_sum = jnp.where((apart == 1) | (apart == CZ - 1), 1.0, 0.0).astype(jnp.bfloat16)

    def middle(src, where, s, dst, to, x, n):
        rates = d_ref[s], k_ref[s]
        substep([(src.at[s], where, half, HALF, x, n, y, *rates) for y in OUTER], up, z_sum)
        substep([(half, HALF, dst.at[s], to, x + 1, n - 2, y, *rates) for y in INNER], up, z_sum)

    def edges(src, where, dst, to, starts):
        rates = [(d_ref[s], k_ref[s]) for s in range(S)]
        between = [[(edge.at[s, side], (-x, 1)) for side, x in enumerate(starts)] for s in range(S)]
        substep(
            [
                (src.at[s], where, *between[s][side], x, 6, y, *rates[s])
                for s in range(S) for side, x in enumerate(starts) for y in OUTER
            ], up, z_sum,
        )
        substep(
            [
                (*between[s][side], dst.at[s], to, x + 1, 4, y, *rates[s])
                for s in range(S) for side, x in enumerate(starts) for y in INNER
            ], up, z_sum,
        )

    for d in both:
        up_y(d).wait_recv()

    def pass_on():
        for d in both:
            up_x(d).wait_recv()
            x_face(0, d).wait_recv()
            x_face(1, d).wait_recv()
        for kind in both:
            for side, d in pairs:
                corner(kind, side, d).start()

    def send_down_first():
        pl.semaphore_wait(below, 1)
        send_along_gx(1)

    def round_one(s, carry):
        for d in both:
            y_face(0, s, d).wait_recv()
        middle(first, FIRST, s, second, SECOND, 1, CX - 2)
        for d in both:
            y_face(1, s, d).start()
        pl.when(jnp.logical_and(is_first, s == SEND_FIRST))(send_down_first)
        pl.when(s == jnp.where(is_first, PASS_ON_FIRST, PASS_ON))(pass_on)
        return carry

    lax.fori_loop(0, S, round_one, 0)

    def round_two(s, carry):
        for d in both:
            y_face(1, s, d).wait_recv()
        middle(second, SECOND, s, out, (0, 0), 3, CX - 6)

        @pl.when(s == BEFORE_EDGES - 1)
        def _():
            for d in both:
                x_face(2, d).wait_recv()
            corners_arrived(0)
            corners_arrived(1)
            edges(first, FIRST, second, SECOND, (-3, CX - 3))
            for side, d in pairs:
                corner(2, side, d).start()

        return carry

    lax.fori_loop(0, S, round_two, 0)
    corners_arrived(2)
    edges(second, SECOND, out, (0, 0), (-1, CX - 5))

    def sent(ref, sem):
        pltpu.make_async_copy(ref, ref, sem).wait()

    for d in both:
        sent(first.at[all_s, pl.ds(0, CX), pl.ds(0, 2)], y_send.at[0, d])
        sent(second.at[all_s, pl.ds(0, CX - 4), pl.ds(0, 2)], y_send.at[1, d])
        sent(first.at[all_s, pl.ds(0, 4), pl.ds(0, CY)], x_send.at[d])
        up_y(d).wait_send()
        up_x(d).wait_send()
    for kind in range(3):
        sent((first.at[all_s, pl.ds(0, 12), pl.ds(0, 2)], up.at[pl.ds(0, 8), pl.ds(0, 1)])[kind % 2], corner_send.at[kind])


def solution(mesh):
    nx, ny = mesh.shape["gx"], mesh.shape["gy"]

    def local(*arrays):
        arrays = [pltpu.with_memory_space_constraint(a, pltpu.HBM) for a in arrays]
        dma = pltpu.SemaphoreType.DMA
        return pl.pallas_call(
            functools.partial(kernel, nx, ny),
            out_shape=jax.ShapeDtypeStruct((S, CX, CY, CZ), jnp.float32),
            in_specs=[pl.BlockSpec(memory_space=pltpu.HBM)] * 4,
            out_specs=pl.BlockSpec(memory_space=pltpu.VMEM),
            scratch_shapes=[
                pltpu.SMEM((S,), jnp.float32),
                pltpu.SMEM((S,), jnp.float32),
                pltpu.VMEM((S, CX + 8, CY + 4, CZ), jnp.float32),
                pltpu.VMEM((S, CX + 4, CY + 4, CZ), jnp.float32),
                pltpu.VMEM((CX + 6, CY + 2, CZ), jnp.float32),
                pltpu.VMEM((S, 2, 6, CY + 2, CZ), jnp.float32),
                pltpu.VMEM((CX + 6, CY + 2, CZ), jnp.float32),
                dma((S + 3,)), dma((2, 2)), dma((2, S, 2)), dma((2,)), dma((3, 2)),
                dma((2, 2)), dma((2, 2)), dma((3,)), dma((3,)),
                pltpu.SemaphoreType.REGULAR, pltpu.SemaphoreType.REGULAR,
            ],
            compiler_params=pltpu.CompilerParams(
                collective_id=0, has_side_effects=True, vmem_limit_bytes=44 << 20
            ),
        )(*arrays)

    placed = (P(None, "gx", "gy", None), P("gx", "gy", None), P(), P())
    return jax.shard_map(
        local, mesh=mesh, in_specs=placed, out_specs=P(None, "gx", "gy", None), check_vma=False
    )
```

time: 102 us -> 27.6 us (0.27)
  the two profiles are of different devices: /device:TPU:0 before, /device:TPU:1 now
where the time goes in v3:
time: 27.6 us; the launch traced here: 27.3 us
  Pallas kernels  25.2 us (91%)
  local copies, waits for them, and re-layouts  2.02 us (7%)
    pallas_call x1, Pallas kernels, local(): pl.pallas_call(functools.partial(kernel, nx, ny), out_shape=jax.ShapeDtyp...  25.2 us
    unnamed x1, local copies, waits for them, and re-layouts  2.02 us

profile of v3, /device:TPU:1, one launch (start us, length us, event | category | flops | bytes accessed | tf_op | source)
XLA Modules:
  0.0 27.3 jit_solution(9239529194931791218)
XLA Ops:
  0.0 25.2 %shard_map.46 = f32[8,64,16,128]{3,2,1,0:T(8,128)S(1)} custom-call(f32[8,64,16,128]{3,2,1,0:T(8,128)} %x_hbm.1, f32[64,16,128]{2,1,0:T(8,128)} %u_hbm.1, f32[8]{0:T(128)} %d_hbm.1, f32[8]{0:T(128)} %k_hbm.1), custom_call_target="tpu_custom_call" | custom-call | tf_op jit(solution)/shard_map/pallas_call | solution.py:252
  25.3 2.0 %copy.6 = f32[8,64,16,128]{3,2,1,0:T(8,128)} copy(f32[8,64,16,128]{3,2,1,0:T(8,128)S(1)} %shard_map.46) | data formatting | bytes 8388608

commit v4 on v3

--- a/solution.py
+++ b/solution.py
@@ -9,10 +9,11 @@
 
 S, CX, CY, CZ = 8, 64, 16, 128
 MESH = pl.DeviceIdType.MESH
-PASS_ON, PASS_ON_FIRST, SEND_FIRST, BEFORE_EDGES = 1, 7, 2, 2
+PASS_ON, PASS_ON_FIRST, SEND_FIRST, BEFORE_EDGES = 1, 4, 2, 2
 
 FIRST, SECOND, HALF, UP = (4, 2), (2, 2), (3, 1), (3, 1)
 OUTER, INNER = (-1, 7, 9), (0, 8)
+OWN, BESIDE = (7,), (-1, 9)
 
 
 def neighbours_in_z(z_sum, center):
@@ -42,8 +43,28 @@
         at(dst, to, x, n, y)[...] = keep * center + rate * total
 
 
+def ones_beside():
+    shape = (2 * CZ, CZ)
+    z, column = (lax.broadcasted_iota(jnp.int32, shape, dim) for dim in (0, 1))
+    apart = lax.rem(z - column + CZ, CZ)
+    return jnp.where((apart == 1) | (apart == CZ - 1), 1.0, 0.0).astype(jnp.bfloat16)
+
+
+def edges(src, where, dst, starts, between, rates, up, z_sum):
+    middle = [[(between.at[s, side], (-x, 1)) for side, x in enumerate(starts)] for s in range(S)]
+    for x_at, n, rows, ends in ((0, 6, OUTER, "out"), (1, 4, INNER, "in")):
+        jobs = []
+        for s in range(S):
+            for side, x in enumerate(starts):
+                source, target = (src.at[s], where), middle[s][side]
+                if ends == "in":
+                    source, target = target, dst(s, side)
+                jobs += [(*source, *target, x + x_at, n, y, *rates[s]) for y in rows]
+        substep(jobs, up, z_sum)
+
+
 def kernel(
-    nx, ny, x_hbm, u_hbm, d_hbm, k_hbm, out, d_ref, k_ref, first, second, half, edge, up,
+    nx, ny, x_hbm, u_hbm, d_hbm, k_hbm, out, second, up, splat, d_ref, k_ref, first, half, edge,
     load_sem, y_send, y_recv, x_send, x_recv, up_send, up_recv, corner_send, corner_recv, above, below,
 ):
     gx, gy = lax.axis_index("gx"), lax.axis_index("gy")
@@ -155,31 +176,23 @@
     load_d.wait()
     load_k.wait()
 
-    apart = lax.rem(
-        lax.broadcasted_iota(jnp.int32, (2 * CZ, CZ), 0) - lax.broadcasted_iota(jnp.int32, (2 * CZ, CZ), 1) + CZ, CZ
-    )
-    z_sum = jnp.where((apart == 1) | (apart == CZ - 1), 1.0, 0.0).astype(jnp.bfloat16)
-
-    def middle(src, where, s, dst, to, x, n):
+    z_sum = ones_beside()
+
+    def ahead(s, carry):
         rates = d_ref[s], k_ref[s]
-        substep([(src.at[s], where, half, HALF, x, n, y, *rates) for y in OUTER], up, z_sum)
-        substep([(half, HALF, dst.at[s], to, x + 1, n - 2, y, *rates) for y in INNER], up, z_sum)
-
-    def edges(src, where, dst, to, starts):
-        rates = [(d_ref[s], k_ref[s]) for s in range(S)]
-        between = [[(edge.at[s, side], (-x, 1)) for side, x in enumerate(starts)] for s in range(S)]
-        substep(
-            [
-                (src.at[s], where, *between[s][side], x, 6, y, *rates[s])
-                for s in range(S) for side, x in enumerate(starts) for y in OUTER
-            ], up, z_sum,
-        )
-        substep(
-            [
-                (*between[s][side], dst.at[s], to, x + 1, 4, y, *rates[s])
-                for s in range(S) for side, x in enumerate(starts) for y in INNER
-            ], up, z_sum,
-        )
+        substep([(first.at[s], FIRST, half.at[s], HALF, 1, CX - 2, y, *rates) for y in OWN], up, z_sum)
+        return carry
+
+    lax.fori_loop(0, S, ahead, 0)
+    for s in range(S):
+        splat[0, s] = jnp.full((8, CZ), d_ref[s])
+        splat[1, s] = jnp.full((8, CZ), k_ref[s])
+
+    def middle(src, where, s, dst, to, x, n, rows):
+        rates = d_ref[s], k_ref[s]
+        between = half.at[s]
+        substep([(src.at[s], where, between, HALF, x, n, y, *rates) for y in rows], up, z_sum)
+        substep([(between, HALF, dst.at[s], to, x + 1, n - 2, y, *rates) for y in INNER], up, z_sum)
 
     for d in both:
         up_y(d).wait_recv()
@@ -200,7 +213,7 @@
     def round_one(s, carry):
         for d in both:
             y_face(0, s, d).wait_recv()
-        middle(first, FIRST, s, second, SECOND, 1, CX - 2)
+        middle(first, FIRST, s, second, SECOND, 1, CX - 2, BESIDE)
         for d in both:
             y_face(1, s, d).start()
         pl.when(jnp.logical_and(is_first, s == SEND_FIRST))(send_down_first)
@@ -212,7 +225,7 @@
     def round_two(s, carry):
         for d in both:
             y_face(1, s, d).wait_recv()
-        middle(second, SECOND, s, out, (0, 0), 3, CX - 6)
+        middle(second, SECOND, s, out, (0, 0), 3, CX - 6, OUTER)
 
         @pl.when(s == BEFORE_EDGES - 1)
         def _():
@@ -220,7 +233,8 @@
                 x_face(2, d).wait_recv()
             corners_arrived(0)
             corners_arrived(1)
-            edges(first, FIRST, second, SECOND, (-3, CX - 3))
+            rates = [(d_ref[s], k_ref[s]) for s in range(S)]
+            edges(first, FIRST, lambda s, side: (second.at[s], SECOND), (-3, CX - 3), edge, rates, up, z_sum)
             for side, d in pairs:
                 corner(2, side, d).start()
 
@@ -228,7 +242,6 @@
 
     lax.fori_loop(0, S, round_two, 0)
     corners_arrived(2)
-    edges(second, SECOND, out, (0, 0), (-1, CX - 5))
 
     def sent(ref, sem):
         pltpu.make_async_copy(ref, ref, sem).wait()
@@ -243,33 +256,59 @@
         sent((first.at[all_s, pl.ds(0, 12), pl.ds(0, 2)], up.at[pl.ds(0, 8), pl.ds(0, 1)])[kind % 2], corner_send.at[kind])
 
 
+def finish(out, second, up, splat, result, edge, rim, sem):
+    inner = [pltpu.make_async_copy(out.at[s, pl.ds(4, CX - 8)], result.at[s, pl.ds(4, CX - 8)], sem.at[s]) for s in range(S)]
+    outer = [
+        pltpu.make_async_copy(rim.at[pl.ds(0, S), side], result.at[pl.ds(0, S), pl.ds(x, 4)], sem.at[S + side])
+        for side, x in enumerate((0, CX - 4))
+    ]
+    for copy in inner:
+        copy.start()
+    rates = [(splat[0, s], splat[1, s]) for s in range(S)]
+    place = ((0, 0), (4 - CX, 0))
+    edges(second, SECOND, lambda s, side: (rim.at[s, side], place[side]), (-1, CX - 5), edge, rates, up, ones_beside())
+    for copy in outer:
+        copy.start()
+    for copy in inner + outer:
+        copy.wait()
+
+
 def solution(mesh):
     nx, ny = mesh.shape["gx"], mesh.shape["gy"]
 
     def local(*arrays):
         arrays = [pltpu.with_memory_space_constraint(a, pltpu.HBM) for a in arrays]
         dma = pltpu.SemaphoreType.DMA
-        return pl.pallas_call(
+        f32, vmem = jnp.float32, pl.BlockSpec(memory_space=pltpu.VMEM)
+        shapes = (S, CX, CY, CZ), (S, CX + 4, CY + 4, CZ), (CX + 6, CY + 2, CZ), (2, S, 8, CZ)
+        between = pltpu.VMEM((S, 2, 6, CY + 2, CZ), f32)
+        parts = pl.pallas_call(
             functools.partial(kernel, nx, ny),
-            out_shape=jax.ShapeDtypeStruct((S, CX, CY, CZ), jnp.float32),
+            out_shape=[jax.ShapeDtypeStruct(shape, f32) for shape in shapes],
             in_specs=[pl.BlockSpec(memory_space=pltpu.HBM)] * 4,
-            out_specs=pl.BlockSpec(memory_space=pltpu.VMEM),
+            out_specs=[vmem] * 4,
             scratch_shapes=[
-                pltpu.SMEM((S,), jnp.float32),
-                pltpu.SMEM((S,), jnp.float32),
-                pltpu.VMEM((S, CX + 8, CY + 4, CZ), jnp.float32),
-                pltpu.VMEM((S, CX + 4, CY + 4, CZ), jnp.float32),
-                pltpu.VMEM((CX + 6, CY + 2, CZ), jnp.float32),
-                pltpu.VMEM((S, 2, 6, CY + 2, CZ), jnp.float32),
-                pltpu.VMEM((CX + 6, CY + 2, CZ), jnp.float32),
+                pltpu.SMEM((S,), f32),
+                pltpu.SMEM((S,), f32),
+                pltpu.VMEM((S, CX + 8, CY + 4, CZ), f32),
+                pltpu.VMEM((S, CX + 6, CY + 2, CZ), f32),
+                between,
                 dma((S + 3,)), dma((2, 2)), dma((2, S, 2)), dma((2,)), dma((3, 2)),
                 dma((2, 2)), dma((2, 2)), dma((3,)), dma((3,)),
                 pltpu.SemaphoreType.REGULAR, pltpu.SemaphoreType.REGULAR,
             ],
             compiler_params=pltpu.CompilerParams(
-                collective_id=0, has_side_effects=True, vmem_limit_bytes=44 << 20
+                collective_id=0, has_side_effects=True, vmem_limit_bytes=40 << 20
             ),
         )(*arrays)
+        return pl.pallas_call(
+            finish,
+            out_shape=jax.ShapeDtypeStruct(shapes[0], f32),
+            in_specs=[vmem] * 4,
+            out_specs=pl.BlockSpec(memory_space=pltpu.HBM),
+            scratch_shapes=[between, pltpu.VMEM((S, 2, 4, CY, CZ), f32), dma((S + 2,))],
+            compiler_params=pltpu.CompilerParams(vmem_limit_bytes=32 << 20),
+        )(*parts)
 
     placed = (P(None, "gx", "gy", None), P("gx", "gy", None), P(), P())
     return jax.shard_map(

time: 27.6 us -> 25.9 us (0.938)
  the two profiles are of different devices: /device:TPU:1 before, /device:TPU:224 now
where the time goes in v4:
time: 25.9 us; the launch traced here: 25.8 us
  Pallas kernels  25.8 us (100%)
    pallas_call x1, Pallas kernels, local(): pl.pallas_call(functools.partial(kernel, nx, ny), out_shape=[jax.ShapeDty...  23.1 us
    pallas_call x1, Pallas kernels, local(): pl.pallas_call(finish, out_shape=jax.ShapeDtypeStruct(shapes[0], f32), in...  2.68 us

profile of v4, /device:TPU:224, one launch (start us, length us, event | category | flops | bytes accessed | tf_op | source)
XLA Modules:
  0.0 25.8 jit_solution(16897900352558704609)
XLA Ops:
  0.0 23.1 %shard_map.46 = (f32[8,64,16,128]{3,2,1,0:T(8,128)S(1)}, f32[8,68,20,128]{3,2,1,0:T(8,128)S(1)}, f32[70,18,128]{2,1,0:T(8,128)S(1)}, f32[2,8,8,128]{3,2,1,0:T(8,128)S(1)}) custom-call(f32[8,64,16,128]{3,2,1,0:T(8,128)} %x_hbm.1, f32[64,16,128]{2,1,0:T(8,128)} %u_hbm.1, f32[8]{0:T(128)} %d_hbm.1, f32[8]{0:T(128)} %k_hbm.1), custom_call_target="tpu_custom_call" | custom-call | tf_op jit(solution)/shard_map/pallas_call | solution.py:285
  23.1 2.7 %shard_map.47 = f32[8,64,16,128]{3,2,1,0:T(8,128)} custom-call(f32[8,64,16,128]{3,2,1,0:T(8,128)S(1)} %get-tuple-element.9.out, f32[8,68,20,128]{3,2,1,0:T(8,128)S(1)} %get-tuple-element.10.second, f32[70,18,128]{2,1,0:T(8,128)S(1)} %get-tuple-element.11.up, f32[2,8,8,128]{3,2,1,0:T(8,128)S(1)} %get-tuple-element.12.splat), custom_call_target="tpu_custom_call" | custom-call | tf_op jit(solution)/shard_map/pallas_call | solution.py:304

commit v5 on v4

--- a/solution.py
+++ b/solution.py
@@ -9,10 +9,11 @@
 
 S, CX, CY, CZ = 8, 64, 16, 128
 MESH = pl.DeviceIdType.MESH
-PASS_ON, PASS_ON_FIRST, SEND_FIRST, BEFORE_EDGES = 1, 4, 2, 2
+PASS_ON, PASS_ON_FIRST, SEND_FIRST, BEFORE_EDGES, BEFORE_EDGES_FIRST = 2, 4, 2, 1, 2
 
 FIRST, SECOND, HALF, UP = (4, 2), (2, 2), (3, 1), (3, 1)
 OUTER, INNER = (-1, 7, 9), (0, 8)
+CHUNK = 1
 OWN, BESIDE = (7,), (-1, 9)
 
 
@@ -34,13 +35,16 @@
 
     centers = [at(src, where, x, n, y)[...] for src, where, _, _, x, n, y, _, _ in jobs]
     sums, done = neighbours_in_z(z_sum, jnp.concatenate(centers, axis=0)), 0
-    for center, (src, where, dst, to, x, n, y, rate, decay) in zip(centers, jobs, strict=True):
-        total = sums[done : done + n]
-        done += n
-        total = total + (at(src, where, x, n, y - 1)[...] + at(src, where, x, n, y + 1)[...])
-        total = total + (at(src, where, x - 1, n, y)[...] + at(src, where, x + 1, n, y)[...])
-        keep = (1.0 - 6.0 * rate) - decay * at(up, UP, x, n, y)[...]
-        at(dst, to, x, n, y)[...] = keep * center + rate * total
+    for src, where, dst, to, first, planes, y, rate, decay in jobs:
+        stay = 1.0 - 6.0 * rate
+        for x in range(first, first + planes, CHUNK):
+            n = min(CHUNK, first + planes - x)
+            total = sums[done : done + n]
+            done += n
+            total = total + (at(src, where, x, n, y - 1)[...] + at(src, where, x, n, y + 1)[...])
+            total = total + (at(src, where, x - 1, n, y)[...] + at(src, where, x + 1, n, y)[...])
+            keep = stay - decay * at(up, UP, x, n, y)[...]
+            at(dst, to, x, n, y)[...] = keep * at(src, where, x, n, y)[...] + rate * total
 
 
 def ones_beside():
@@ -188,11 +192,16 @@
         splat[0, s] = jnp.full((8, CZ), d_ref[s])
         splat[1, s] = jnp.full((8, CZ), k_ref[s])
 
-    def middle(src, where, s, dst, to, x, n, rows):
-        rates = d_ref[s], k_ref[s]
-        between = half.at[s]
-        substep([(src.at[s], where, between, HALF, x, n, y, *rates) for y in rows], up, z_sum)
-        substep([(between, HALF, dst.at[s], to, x + 1, n - 2, y, *rates) for y in INNER], up, z_sum)
+    def one(src, where, s, x, n, rows):
+        return [(src.at[s], where, half.at[s], HALF, x, n, y, d_ref[s], k_ref[s]) for y in rows]
+
+    def two(s, dst, to, x, n):
+        return [(half.at[s], HALF, dst.at[s], to, x, n, y, d_ref[s], k_ref[s]) for y in INNER]
+
+    one_first = lambda s: one(first, FIRST, s, 1, CX - 2, BESIDE)
+    two_first = lambda s: two(s, second, SECOND, 2, CX - 4)
+    one_second = lambda s: one(second, SECOND, s, 3, CX - 6, OUTER)
+    two_second = lambda s: two(s, out, (0, 0), 4, CX - 8)
 
     for d in both:
         up_y(d).wait_recv()
@@ -210,37 +219,48 @@
         pl.semaphore_wait(below, 1)
         send_along_gx(1)
 
+    def arrived(r, s):
+        for d in both:
+            y_face(r, s, d).wait_recv()
+
+    def send_second(s):
+        for d in both:
+            y_face(1, s, d).start()
+
     def round_one(s, carry):
-        for d in both:
-            y_face(0, s, d).wait_recv()
-        middle(first, FIRST, s, second, SECOND, 1, CX - 2, BESIDE)
-        for d in both:
-            y_face(1, s, d).start()
+        arrived(0, s)
+        substep(two_first(s - 1) + one_first(s), up, z_sum)
+        send_second(s - 1)
         pl.when(jnp.logical_and(is_first, s == SEND_FIRST))(send_down_first)
         pl.when(s == jnp.where(is_first, PASS_ON_FIRST, PASS_ON))(pass_on)
         return carry
 
-    lax.fori_loop(0, S, round_one, 0)
+    arrived(0, 0)
+    substep(one_first(0), up, z_sum)
+    lax.fori_loop(1, S, round_one, 0)
+    substep(two_first(S - 1), up, z_sum)
+    send_second(S - 1)
+
+    def edges_between():
+        for d in both:
+            x_face(2, d).wait_recv()
+        corners_arrived(0)
+        corners_arrived(1)
+        rates = [(d_ref[s], k_ref[s]) for s in range(S)]
+        edges(first, FIRST, lambda s, side: (second.at[s], SECOND), (-3, CX - 3), edge, rates, up, z_sum)
+        for side, d in pairs:
+            corner(2, side, d).start()
 
     def round_two(s, carry):
-        for d in both:
-            y_face(1, s, d).wait_recv()
-        middle(second, SECOND, s, out, (0, 0), 3, CX - 6, OUTER)
-
-        @pl.when(s == BEFORE_EDGES - 1)
-        def _():
-            for d in both:
-                x_face(2, d).wait_recv()
-            corners_arrived(0)
-            corners_arrived(1)
-            rates = [(d_ref[s], k_ref[s]) for s in range(S)]
-            edges(first, FIRST, lambda s, side: (second.at[s], SECOND), (-3, CX - 3), edge, rates, up, z_sum)
-            for side, d in pairs:
-                corner(2, side, d).start()
-
+        arrived(1, s)
+        substep(two_second(s - 1) + one_second(s), up, z_sum)
+        pl.when(s == jnp.where(is_first, BEFORE_EDGES_FIRST, BEFORE_EDGES))(edges_between)
         return carry
 
-    lax.fori_loop(0, S, round_two, 0)
+    arrived(1, 0)
+    substep(one_second(0), up, z_sum)
+    lax.fori_loop(1, S, round_two, 0)
+    substep(two_second(S - 1), up, z_sum)
     corners_arrived(2)
 
     def sent(ref, sem):

time: 25.9 us -> 24.5 us (0.946)
  Pallas kernels: 25.8 us -> 24.4 us
    pallas_call x1, Pallas kernels: 23.1 us -> 22.4 us  [local(): pl.pallas_call(functools.partial(kernel, nx, ny), out_shape=[jax.ShapeDty...]
    pallas_call x1, Pallas kernels: 2.68 us -> 2.09 us  [local(): pl.pallas_call(finish, out_shape=jax.ShapeDtypeStruct(shapes[0], f32), in...]
where the time goes in v5:
time: 24.5 us
  Pallas kernels  24.4 us (100%)
    pallas_call x1, Pallas kernels, local(): pl.pallas_call(functools.partial(kernel, nx, ny), out_shape=[jax.ShapeDty...  22.4 us
    pallas_call x1, Pallas kernels, local(): pl.pallas_call(finish, out_shape=jax.ShapeDtypeStruct(shapes[0], f32), in...  2.09 us

profile of v5, /device:TPU:224, one launch (start us, length us, event | category | flops | bytes accessed | tf_op | source)
XLA Modules:
  0.0 24.5 jit_solution(17407936569894690796)
XLA Ops:
  0.0 22.4 %shard_map.46 = (f32[8,64,16,128]{3,2,1,0:T(8,128)S(1)}, f32[8,68,20,128]{3,2,1,0:T(8,128)S(1)}, f32[70,18,128]{2,1,0:T(8,128)S(1)}, f32[2,8,8,128]{3,2,1,0:T(8,128)S(1)}) custom-call(f32[8,64,16,128]{3,2,1,0:T(8,128)} %x_hbm.1, f32[64,16,128]{2,1,0:T(8,128)} %u_hbm.1, f32[8]{0:T(128)} %d_hbm.1, f32[8]{0:T(128)} %k_hbm.1), custom_call_target="tpu_custom_call" | custom-call | tf_op jit(solution)/shard_map/pallas_call | solution.py:305
  22.4 2.1 %shard_map.47 = f32[8,64,16,128]{3,2,1,0:T(8,128)} custom-call(f32[8,64,16,128]{3,2,1,0:T(8,128)S(1)} %get-tuple-element.9.out, f32[8,68,20,128]{3,2,1,0:T(8,128)S(1)} %get-tuple-element.10.second, f32[70,18,128]{2,1,0:T(8,128)S(1)} %get-tuple-element.11.up, f32[2,8,8,128]{3,2,1,0:T(8,128)S(1)} %get-tuple-element.12.splat), custom_call_target="tpu_custom_call" | custom-call | tf_op jit(solution)/shard_map/pallas_call | solution.py:324
